TPU v7x, 256 devices: a whole 4x4x8 slice. The times are simulated.
256 devices in a mesh: freq: 2 (over core), row: 8 (over y_hi, x), col: 16 (over z, y_lo).
Axes of the slice: x: 4, y: 4 (y_hi: 2, y_lo: 2; y = y_hi * 2 + y_lo), z: 8, core: 2. Of those that a mesh axis runs over, the one named last changes fastest.
Arguments:
- coupling: bfloat16 [12288, 6144], P('row', 'col'), may hold values from -0.109375 to 0.109375
- freq_weight: float32 [24576], P(('freq', 'row')), parts along dimension 0, may hold values from 0.05 to 2
Outputs:
- response: float32 [12288, 6144], P(('freq', 'row'), 'col'), parts along dimension 0
There are 2 independent parts, one for each index of `freq`. A program takes and returns all parts, laid end to end along the dimension named above; an argument that names none is the same for every part. Nothing has to cross between parts.
All inputs are finite; a program needn't handle non-finite values.
Results may differ from a plain program's by a relative error of at most 0.0021.
Values may be sent and summed in bfloat16 or wider, within the bound.
No kernel may reach another device: no remote copies, remote signals or barrier semaphores. Data moves between devices by JAX's collectives and lax.ppermute only.
A program may use at most 128 MiB of HBM per device.

v0:
```python
import jax
import jax.numpy as jnp
from jax import lax
from jax.sharding import Mesh
from jax.sharding import PartitionSpec as P

COL = ("col_0", "col_1")


def gather_axes(x, axes, dim):
    whole = x
    for number in range(len(axes) - 1, -1, -1):
        whole = lax.all_gather(whole, axes[number], axis=dim, tiled=True)
    return whole


def on_device(coupling, freq_weight):
    weighted = (coupling.astype(jnp.float32) * freq_weight[:, None]).astype(jnp.bfloat16)
    full_rows = gather_axes(weighted, COL, 1)
    return lax.psum_scatter(
        lax.dot_general(
            full_rows, coupling, (((0,), (0,)), ((), ())), preferred_element_type=jnp.float32
        ),
        "row",
        scatter_dimension=0,
        tiled=True,
    )


def solution(mesh):
    torus = Mesh(
        mesh.devices.reshape(mesh.shape["freq"], mesh.shape["row"], 8, 2),
        ("freq", "row", "col_0", "col_1"),
    )
    placed = (P("row", COL), P(("freq", "row")))
    return jax.shard_map(
        on_device, mesh=torus, in_specs=placed, out_specs=P(("freq", "row"), COL), check_vma=False
    )
```

profile of v0, /device:TPU:1, one launch (start us, length us, event | category | flops | bytes accessed | tf_op | source)
XLA Modules:
  0.0 397.5 jit_solution(10122564019564711897)
XLA Ops:
  6.5 0.0 all-gather.3.cloned.1.call-start
  6.5 2.6 multiply_convert_fusion
  9.1 0.0 copy-start
  9.1 0.0 all-gather.3.cloned.1.call-update
  9.1 0.0 all-gather.5.cloned.1.call-start
  9.2 44.9 %all-gather.3.cloned.1.call-done = bf16[1536,768]{1,0:T(8,128)(2,1)} async-done(((bf16[1536,384]{1,0:T(8,128)(2,1)}), bf16[1536,768]{1,0:T(8,128)(2,1)}) %all-gather.3.cloned.1.call-update) | async-done | bytes 2359312 | tf_op jit(solution)/shard_map/all_gather | solution.py:13
  54.0 0.0 all-gather.5.cloned.1.call-update
  54.1 0.0 reduce-scatter.2.cloned.1.call-start
  54.1 195.1 %all-gather.5.cloned.1.call-done = bf16[1536,6144]{1,0:T(8,128)(2,1)} async-done(((bf16[1536,768]{1,0:T(8,128)(2,1)}), bf16[1536,6144]{1,0:T(8,128)(2,1)}) %all-gather.5.cloned.1.call-update) | async-done | bytes 18874384 | tf_op jit(solution)/shard_map/all_gather | solution.py:13
  249.2 0.0 copy-done
  249.2 16.2 %fusion = f32[6144,384]{1,0:T(8,128)} fusion(bf16[1536,6144]{1,0:T(8,128)(2,1)} %all-gather.5.cloned.1.call-done, bf16[1536,384]{1,0:T(8,128)(2,1)S(1)} %copy-done), kind=kOutput, calls=%fused_computation.1 | convolution fusion | flops 7247757312 | bytes 29491200 | tf_op jit(solution)/shard_map/dot_general | solution.py:21
  265.4 0.0 reduce-scatter.2.cloned.1.call-update
  265.4 125.5 %reduce-scatter.2.cloned.1.call-done = f32[768,384]{1,0:T(8,128)} async-done(((f32[6144,384]{1,0:T(8,128)}), f32[768,384]{1,0:T(8,128)}) %reduce-scatter.2.cloned.1.call-update) | async-done | bytes 1179664 | tf_op jit(solution)/shard_map/reduce_scatter | solution.py:20
Async XLA Ops:
  6.5 47.5 %all-gather.3.cloned.1.call-start = ((), (), s32[]{:S(2)}) async-start(), calls=%async_computation.1 | async-start | bytes 3538944 | tf_op jit(solution)/shard_map/all_gather | solution.py:13
  9.1 240.2 %copy-start = (bf16[1536,384]{1,0:T(8,128)(2,1)S(1)}, bf16[1536,384]{1,0:T(8,128)(2,1)}, u32[]{:S(2)}) copy-start(bf16[1536,384]{1,0:T(8,128)(2,1)} %param.2) | copy-start | bytes 3538948
  9.1 240.1 %all-gather.5.cloned.1.call-start = ((), (), s32[]{:S(2)}) async-start(), calls=%async_computation.2 | async-start | bytes 21233664 | tf_op jit(solution)/shard_map/all_gather | solution.py:13
  54.1 336.9 %reduce-scatter.2.cloned.1.call-start = ((), (), s32[]{:S(2)}) async-start(), calls=%async_computation.3 | async-start | bytes 10616832 | tf_op jit(solution)/shard_map/reduce_scatter | solution.py:20
Sparse Core Ops, SparseCore 0:
  9.2 44.7 all-gather.2
  55.8 193.3 all-gather.4
  265.5 125.3 reduce-scatter.1
where the time goes:
time: 398 us; the launch traced here: 397 us
  waiting for transfers between devices  366 us (92%)
  matrix products  16.2 us (4%)
  between operations  13.1 us (3%)
    all_gather x2, waiting for transfers between devices, gather_axes(): whole = lax.all_gather(whole, axes[number], axis=dim, tiled=True)  240 us
    reduce_scatter x1, waiting for transfers between devices, on_device(): lax.psum_scatter(lax.dot_general(full_rows, coupling, (((0,), (0,)), ((),...  126 us
    dot_general x1, matrix products, on_device(): lax.dot_general(full_rows, coupling, (((0,), (0,)), ((), ())), preferred_...  16.2 us
  transfers between devices with their start and end apart: 3, of which 3 were waited for; matrix products, arithmetic and copies ran while one was open for 0% of the time, Pallas kernels for 0%

commit v1 on v0

v1 whole, which is shorter than its diff:
```python
import jax
import jax.numpy as jnp
from jax import lax
from jax.sharding import Mesh
from jax.sharding import PartitionSpec as P

FREQ, YH, X, Z, YL = 2, 2, 4, 8, 2
AXES = ("f", "yh", "x", "z", "yl")
CHUNKS = 3


def place(f, yh, x, z, yl):
    return (((f * YH + yh) * X + x) * Z + z) * YL + yl


def ring_pairs(size, sign, cores=(0, 1)):
    pairs = []
    for f in cores:
        step = sign if f == 0 else -sign
        pairs += [(f * size + i, f * size + (i + step) % size) for i in range(size)]
    return pairs


def home_yh(f, x, z, late):
    j = (z - x) % X if f == 0 else (x - z) % X
    if j == 0 and f == late:
        j = X
    r = (z - j if f == 0 else z + j) % Z
    return r // X


def y_pairs(k1, k0, late):
    pairs = []
    for f in range(FREQ):
        for yh in range(YH):
            for x in range(X):
                for z in range(Z):
                    for yl in range(YL):
                        there = place(yh ^ k1, home_yh(f, x, z, late), x, z, yl ^ k0)
                        pairs.append((place(f, yh, x, z, yl), there))
    return pairs


def on_device(coupling, freq_weight):
    f, yh, x, z, yl = (lax.axis_index(a) for a in AXES)
    rows, cols = coupling.shape
    width = cols // CHUNKS
    other_weight = lax.ppermute(freq_weight, "f", [(0, 1), (1, 0)])
    weight = [
        jnp.where(f == 0, freq_weight, other_weight)[:, None],
        jnp.where(f == 0, other_weight, freq_weight)[:, None],
    ]
    beside = lax.ppermute(coupling, "yl", [(0, 1), (1, 0)])
    right = jnp.concatenate([coupling, beside], axis=1)
    first = jnp.where(f == 0, z - x, x - z) % X
    blocks = []
    for c in range(CHUNKS):
        late = 1 - c % 2
        own = coupling[:, c * width : (c + 1) * width]
        held = [own]
        for step in range(4):
            cores = (0, 1) if step < 3 else (late,)
            held.append(lax.ppermute(held[-1], ("f", "z"), ring_pairs(Z, 1, cores)))
        slots = [jnp.where(f == late, held[4], own)] + held[1:4]

        def product(delta):
            at = (first - delta) % X
            tile = jnp.where(
                at < 2,
                jnp.where(at == 0, slots[0], slots[1]),
                jnp.where(at == 2, slots[2], slots[3]),
            ).astype(jnp.float32)
            left = jnp.concatenate(
                [(tile * w).astype(jnp.bfloat16) for w in weight], axis=1
            )
            return lax.dot_general(
                left, right, (((0,), (0,)), ((), ())), preferred_element_type=jnp.float32
            )

        relay = lax.ppermute(product(2).astype(jnp.bfloat16), ("f", "x"), ring_pairs(X, 1))
        back = lax.ppermute(product(3).astype(jnp.bfloat16), ("f", "x"), ring_pairs(X, -1))
        ahead = (product(1) + relay.astype(jnp.float32)).astype(jnp.bfloat16)
        ahead = lax.ppermute(ahead, ("f", "x"), ring_pairs(X, 1))
        total = product(0) + back.astype(jnp.float32) + ahead.astype(jnp.float32)
        total = total.astype(jnp.bfloat16).reshape(FREQ, width, YL, cols)
        halves = []
        for k0 in range(YL):
            parts = []
            for k1 in range(YH):
                piece = jnp.where(yh == k1, total[0, :, k0], total[1, :, k0])
                parts.append(lax.ppermute(piece, AXES, y_pairs(k1, k0, late)))
            halves.append(parts[0].astype(jnp.float32) + parts[1].astype(jnp.float32))
        blocks.append(halves)
    even = [jnp.where(yl == 0, h[0], h[1]) for h in blocks]
    odd = [jnp.where(yl == 0, h[1], h[0]) for h in blocks]
    return jnp.concatenate(even + odd, axis=0)


def solution(mesh):
    torus = Mesh(mesh.devices.reshape(FREQ, YH, X, Z, YL), AXES)
    placed = (P(("yh", "x"), ("z", "yl")), P(("f", "yh", "x")))
    return jax.shard_map(
        on_device,
        mesh=torus,
        in_specs=placed,
        out_specs=P(("f", "yh", "x"), ("z", "yl")),
        check_vma=False,
    )
```

time: 398 us -> 142 us (0.36)
  waiting for transfers between devices: 366 us -> 20.1 us
  starting transfers between devices: 0.08 us -> 84.7 us
  between operations: 13.1 us -> 0.46 us
  other arithmetic: 2.56 us -> 11.4 us
  local copies, waits for them, and re-layouts: 0.01 us -> 8.42 us
    all_gather x2 -> x0, waiting for transfers between devices: 240 us -> none  [gather_axes(): whole = lax.all_gather(whole, axes[number], axis=dim, tiled=True)]
    reduce_scatter x1 -> x0, waiting for transfers between devices: 126 us -> none  [on_device(): lax.psum_scatter(lax.dot_general(full_rows, coupling, (((0,), (0,)), ((),...]
    ppermute x0 -> x35, starting transfers between devices: none -> 84.7 us  [the longest x12 36.9 us: on_device(): held.append(lax.ppermute(held[-1], ('f', 'z'), ring_pairs(Z, 1, cores)))]
    ppermute x0 -> x35, waiting for transfers between devices: none -> 20.1 us  [the longest x12 11.4 us: on_device(): held.append(lax.ppermute(held[-1], ('f', 'z'), ring_pairs(Z, 1, cores)))]
    convert_element_type x1 -> x5, other arithmetic: 2.56 us -> 7.71 us  [product(): (tile * w).astype(jnp.bfloat16)]
    dot_general x1 -> x12, matrix products: 16.2 us -> 15.8 us  [product(): lax.dot_general(left, right, (((0,), (0,)), ((), ())), preferred_element_...]
  transfers between devices with their start and end apart: 3 -> 35, of which waited for: 3 -> 12; matrix products, arithmetic and copies ran while one was open for 0% -> 16% of each run, Pallas kernels for 0% -> 0%
where the time goes in v1:
time: 142 us; the launch traced here: 141 us
  starting transfers between devices  84.7 us (60%)
  waiting for transfers between devices  20.1 us (14%)
  matrix products  15.8 us (11%)
  other arithmetic  11.4 us (8%)
  local copies, waits for them, and re-layouts  8.42 us (6%)
    ppermute x12, starting transfers between devices, on_device(): held.append(lax.ppermute(held[-1], ('f', 'z'), ring_pairs(Z, 1, cores)))  36.9 us
    ppermute x12, starting transfers between devices, on_device(): parts.append(lax.ppermute(piece, AXES, y_pairs(k1, k0, late)))  31.3 us
    dot_general x12, matrix products, product(): lax.dot_general(left, right, (((0,), (0,)), ((), ())), preferred_element_...  15.8 us
    ppermute x12, waiting for transfers between devices, on_device(): held.append(lax.ppermute(held[-1], ('f', 'z'), ring_pairs(Z, 1, cores)))  11.4 us
    convert_element_type x5, other arithmetic, product(): (tile * w).astype(jnp.bfloat16)  7.71 us
    ppermute x3, starting transfers between devices, on_device(): lax.ppermute(product(2).astype(jnp.bfloat16), ('f', 'x'), ring_pairs(X, 1))  7.52 us
    ppermute x3, waiting for transfers between devices, on_device(): lax.ppermute(product(2).astype(jnp.bfloat16), ('f', 'x'), ring_pairs(X, 1))  6.53 us
    ppermute x3, starting transfers between devices, on_device(): ahead = lax.ppermute(ahead, ('f', 'x'), ring_pairs(X, 1))  6.34 us
  transfers between devices with their start and end apart: 35, of which 12 were waited for; matrix products, arithmetic and copies ran while one was open for 16% of the time, Pallas kernels for 0%

profile of v1, /device:TPU:1, one launch (start us, length us, event | category | flops | bytes accessed | tf_op | source)
XLA Modules:
  0.0 141.0 jit_solution(7254125663296223682)
XLA Ops:
  1.4 6.5 %collective-permute-start.13 = (bf16[1536,128]{1,0:T(8,128)(2,1)S(1)}, bf16[1536,128]{1,0:T(8,128)(2,1)S(1)}, u32[]{:S(2)}, u32[]{:S(2)}) collective-permute-start(bf16[1536,128]{1,0:T(8,128)(2,1)S(1)} %get-tuple-element.49), channel_id=1, source_target_pairs={{0,2},{2,4},{4,6},{6,8},{8,10},{10,12},{12,14},{14,0},{128,142},{1... | collective-permute-start | bytes 1179656 | tf_op jit(solution)/shard_map/ppermute | solution.py:63
  12.6 3.1 %collective-permute-start.14 = (bf16[1536,128]{1,0:T(8,128)(2,1)S(1)}, bf16[1536,128]{1,0:T(8,128)(2,1)}, u32[]{:S(2)}, u32[]{:S(2)}) collective-permute-start(bf16[1536,128]{1,0:T(8,128)(2,1)S(1)} %collective-permute-done.13), channel_id=1, source_target_pairs={{0,2},{2,4},{4,6},{6,8},{8,10},{10,12},{12,14},{14,0},{128,142},{1... | collective-permute-start | bytes 1179656 | tf_op jit(solution)/shard_map/ppermute | solution.py:63
  16.8 3.1 %collective-permute-start.25 = (bf16[1536,128]{1,0:T(8,128)(2,1)S(1)}, bf16[1536,128]{1,0:T(8,128)(2,1)S(1)}, u32[]{:S(2)}, u32[]{:S(2)}) collective-permute-start(bf16[1536,128]{1,0:T(8,128)(2,1)S(1)} %collective-permute-done.24), channel_id=1, source_target_pairs={{0,2},{2,4},{4,6},{6,8},{8,10},{10,12},{12,14},{14,0},{128,142},{1... | collective-permute-start | bytes 1179656 | tf_op jit(solution)/shard_map/ppermute | solution.py:63
  21.0 3.1 %collective-permute-start.1 = (bf16[1536,128]{1,0:T(8,128)(2,1)S(1)}, bf16[1536,128]{1,0:T(8,128)(2,1)S(1)}, u32[]{:S(2)}, u32[]{:S(2)}) collective-permute-start(bf16[1536,128]{1,0:T(8,128)(2,1)S(1)} %collective-permute-done), channel_id=1, source_target_pairs={{0,2},{2,4},{4,6},{6,8},{8,10},{10,12},{12,14},{14,0},{128,142},{1... | collective-permute-start | bytes 1179656 | tf_op jit(solution)/shard_map/ppermute | solution.py:63
  25.2 3.2 %collective-permute-start.15 = (bf16[1536,128]{1,0:T(8,128)(2,1)}, bf16[1536,128]{1,0:T(8,128)(2,1)}, u32[]{:S(2)}, u32[]{:S(2)}) collective-permute-start(bf16[1536,128]{1,0:T(8,128)(2,1)} %collective-permute-done.14), channel_id=1, source_target_pairs={{0,2},{2,4},{4,6},{6,8},{8,10},{10,12},{12,14},{14,0},{128,142},{1... | collective-permute-start | bytes 1179656 | tf_op jit(solution)/shard_map/ppermute | solution.py:63
  29.5 3.1 %collective-permute-start.26 = (bf16[1536,128]{1,0:T(8,128)(2,1)S(1)}, bf16[1536,128]{1,0:T(8,128)(2,1)S(1)}, u32[]{:S(2)}, u32[]{:S(2)}) collective-permute-start(bf16[1536,128]{1,0:T(8,128)(2,1)S(1)} %collective-permute-done.25), channel_id=1, source_target_pairs={{0,2},{2,4},{4,6},{6,8},{8,10},{10,12},{12,14},{14,0},{128,142},{1... | collective-permute-start | bytes 1179656 | tf_op jit(solution)/shard_map/ppermute | solution.py:63
  33.7 3.1 %collective-permute-start.2 = (bf16[1536,128]{1,0:T(8,128)(2,1)S(1)}, bf16[1536,128]{1,0:T(8,128)(2,1)S(1)}, u32[]{:S(2)}, u32[]{:S(2)}) collective-permute-start(bf16[1536,128]{1,0:T(8,128)(2,1)S(1)} %collective-permute-done.1), channel_id=1, source_target_pairs={{0,2},{2,4},{4,6},{6,8},{8,10},{10,12},{12,14},{14,0},{128,142},{1... | collective-permute-start | bytes 1179656 | tf_op jit(solution)/shard_map/ppermute | solution.py:63
  38.8 3.3 %collective-permute-done.26 = bf16[1536,128]{1,0:T(8,128)(2,1)S(1)} collective-permute-done((bf16[1536,128]{1,0:T(8,128)(2,1)S(1)}, bf16[1536,128]{1,0:T(8,128)(2,1)S(1)}, u32[]{:S(2)}, u32[]{:S(2)}) %collective-permute-start.26) | collective-permute-done | bytes 393248 | tf_op jit(solution)/shard_map/ppermute | solution.py:63
  42.1 5.0 %collective-permute-start.27 = (bf16[1536,128]{1,0:T(8,128)(2,1)S(1)}, bf16[1536,128]{1,0:T(8,128)(2,1)S(1)}, u32[]{:S(2)}, u32[]{:S(2)}) collective-permute-start(bf16[1536,128]{1,0:T(8,128)(2,1)S(1)} %collective-permute-done.26), channel_id=1, source_target_pairs={{128,142},{130,128},{132,130},{134,132},{136,134},{138,136},{140,1... | collective-permute-start | bytes 1179656 | tf_op jit(solution)/shard_map/ppermute | solution.py:63
  47.1 4.4 %collective-permute-start.3 = (bf16[1536,128]{1,0:T(8,128)(2,1)S(1)}, bf16[1536,128]{1,0:T(8,128)(2,1)S(1)}, u32[]{:S(2)}, u32[]{:S(2)}) collective-permute-start(bf16[1536,128]{1,0:T(8,128)(2,1)S(1)} %collective-permute-done.2), channel_id=1, source_target_pairs={{128,142},{130,128},{132,130},{134,132},{136,134},{138,136},{140,1... | collective-permute-start | bytes 1179656 | tf_op jit(solution)/shard_map/ppermute | solution.py:63
  51.5 2.5 %constant_dynamic-update-slice_fusion = bf16[1536,768]{1,0:T(8,128)(2,1)} fusion(bf16[1536,768]{1,0:T(8,128)(2,1)} %constant_dynamic-update-slice_fusion.1, bf16[1536,384]{1,0:T(8,128)(2,1)} %collective-permute-done.5), kind=kLoop, calls=%fused_computation.144 | loop fusion | bytes 2359296 | tf_op jit(solution)/shard_map/concatenate | solution.py:54
  69.4 2.8 %collective-permute-start.18 = (bf16[256,768]{1,0:T(8,128)(2,1)S(1)}, bf16[256,768]{1,0:T(8,128)(2,1)S(1)}, u32[]{:S(2)}, u32[]{:S(2)}) collective-permute-start(bf16[256,768]{1,0:T(8,128)(2,1)S(1)} %convolution_convert_fusion.2), channel_id=1, source_target_pairs={{0,16},{16,32},{32,48},{48,0},{128,176},{144,128},{160,144},{176,1... | collective-permute-start | bytes 1179656 | tf_op jit(solution)/shard_map/ppermute | solution.py:80
  75.8 3.2 %collective-permute-start.7 = (bf16[256,768]{1,0:T(8,128)(2,1)S(1)}, bf16[256,768]{1,0:T(8,128)(2,1)S(1)}, u32[]{:S(2)}, u32[]{:S(2)}) collective-permute-start(bf16[256,768]{1,0:T(8,128)(2,1)S(1)} %convolution_convert_fusion.4), channel_id=1, source_target_pairs={{0,16},{16,32},{32,48},{48,0},{128,176},{144,128},{160,144},{176,1... | collective-permute-start | bytes 1179656 | tf_op jit(solution)/shard_map/ppermute | solution.py:80
  79.9 4.4 %collective-permute-done.18 = bf16[256,768]{1,0:T(8,128)(2,1)S(1)} collective-permute-done((bf16[256,768]{1,0:T(8,128)(2,1)S(1)}, bf16[256,768]{1,0:T(8,128)(2,1)S(1)}, u32[]{:S(2)}, u32[]{:S(2)}) %collective-permute-start.18) | collective-permute-done | bytes 393248 | tf_op jit(solution)/shard_map/ppermute | solution.py:80
  84.3 3.2 %collective-permute-start.30 = (bf16[256,768]{1,0:T(8,128)(2,1)S(1)}, bf16[256,768]{1,0:T(8,128)(2,1)S(1)}, u32[]{:S(2)}, u32[]{:S(2)}) collective-permute-start(bf16[256,768]{1,0:T(8,128)(2,1)S(1)} %fusion.8), channel_id=1, source_target_pairs={{0,16},{16,32},{32,48},{48,0},{128,176},{144,128},{160,144},{176,1... | collective-permute-start | bytes 1179656 | tf_op jit(solution)/shard_map/ppermute | solution.py:83
  89.9 3.1 %collective-permute-start.19 = (bf16[256,768]{1,0:T(8,128)(2,1)}, bf16[256,768]{1,0:T(8,128)(2,1)}, u32[]{:S(2)}, u32[]{:S(2)}) collective-permute-start(bf16[256,768]{1,0:T(8,128)(2,1)} %fusion.6), channel_id=1, source_target_pairs={{0,16},{16,32},{32,48},{48,0},{128,176},{144,128},{160,144},{176,1... | collective-permute-start | bytes 1179656 | tf_op jit(solution)/shard_map/ppermute | solution.py:83
  96.8 5.2 %collective-permute-start.33 = (bf16[128,384]{1,0:T(8,128)(2,1)}, bf16[128,384]{1,0:T(8,128)(2,1)}, u32[]{:S(2)}, u32[]{:S(2)}) collective-permute-start(bf16[128,384]{1,0:T(8,128)(2,1)} %get-tuple-element.50), channel_id=1, source_target_pairs={{0,1},{1,0},{2,3},{3,2},{4,5},{5,4},{6,7},{7,6},{8,73},{9,72},{10,... | collective-permute-start | bytes 294920 | tf_op jit(solution)/shard_map/ppermute | solution.py:91
  105.1 2.6 %fusion.3 = bf16[256,768]{1,0:T(8,128)(2,1)S(1)} fusion(bf16[1536,768]{1,0:T(8,128)(2,1)} %constant_dynamic-update-slice_fusion, bf16[1536,128]{1,0:T(8,128)(2,1)S(1)} %copy-done.6, bf16[1536,128]{1,0:T(8,128)(2,1)S(1)} %copy-done.4, bf16[256,768]{1,0:T(8,128)(2,1)} %collective-permute-done.8, bf16[256,768]{1,0:T(8,128)(2,1)} %collective-permute-done.6), kind=kOutput, calls=%fused_computation.9 | convolution fusion | flops 606535680 | bytes 4325376 | tf_op jit(solution)/shard_map/dot_general | solution.py:76
  108.5 4.1 %collective-permute-start.11 = (bf16[128,384]{1,0:T(8,128)(2,1)S(1)}, bf16[128,384]{1,0:T(8,128)(2,1)S(1)}, u32[]{:S(2)}, u32[]{:S(2)}) collective-permute-start(bf16[128,384]{1,0:T(8,128)(2,1)S(1)} %get-tuple-element.66), channel_id=1, source_target_pairs={{0,1},{1,0},{2,3},{3,2},{4,5},{5,4},{6,7},{7,6},{8,73},{9,72},{10,... | collective-permute-start | bytes 294920 | tf_op jit(solution)/shard_map/ppermute | solution.py:91
  112.6 3.2 %collective-permute-start.10 = (bf16[128,384]{1,0:T(8,128)(2,1)S(1)}, bf16[128,384]{1,0:T(8,128)(2,1)S(1)}, u32[]{:S(2)}, u32[]{:S(2)}) collective-permute-start(bf16[128,384]{1,0:T(8,128)(2,1)S(1)} %get-tuple-element.73), channel_id=1, source_target_pairs={{0,128},{1,129},{2,130},{3,131},{4,132},{5,133},{6,134},{7,135},{8... | collective-permute-start | bytes 294920 | tf_op jit(solution)/shard_map/ppermute | solution.py:91
  115.8 4.0 %collective-permute-start.9 = (bf16[128,384]{1,0:T(8,128)(2,1)S(1)}, bf16[128,384]{1,0:T(8,128)(2,1)S(1)}, u32[]{:S(2)}, u32[]{:S(2)}) collective-permute-start(bf16[128,384]{1,0:T(8,128)(2,1)S(1)} %get-tuple-element.72), channel_id=1, source_target_pairs={{0,0},{1,1},{2,2},{3,3},{4,4},{5,5},{6,6},{7,7},{8,72},{9,73},{10,... | collective-permute-start | bytes 294920 | tf_op jit(solution)/shard_map/ppermute | solution.py:91
  121.8 3.3 %collective-permute-start.20 = (bf16[128,384]{1,0:T(8,128)(2,1)S(1)}, bf16[128,384]{1,0:T(8,128)(2,1)S(1)}, u32[]{:S(2)}, u32[]{:S(2)}) collective-permute-start(bf16[128,384]{1,0:T(8,128)(2,1)S(1)} %get-tuple-element.64), channel_id=1, source_target_pairs={{0,64},{1,65},{2,2},{3,3},{4,4},{5,5},{6,6},{7,7},{8,8},{9,9},{10,... | collective-permute-start | bytes 294920 | tf_op jit(solution)/shard_map/ppermute | solution.py:91
  125.8 4.0 %collective-permute-start.34 = (bf16[128,384]{1,0:T(8,128)(2,1)S(1)}, bf16[128,384]{1,0:T(8,128)(2,1)S(1)}, u32[]{:S(2)}, u32[]{:S(2)}) collective-permute-start(bf16[128,384]{1,0:T(8,128)(2,1)S(1)} %copy-done.8), channel_id=1, source_target_pairs={{0,129},{1,128},{2,131},{3,130},{4,133},{5,132},{6,135},{7,134},{8... | collective-permute-start | bytes 294920 | tf_op jit(solution)/shard_map/ppermute | solution.py:91
  129.8 3.2 %collective-permute-start.31 = (bf16[128,384]{1,0:T(8,128)(2,1)S(1)}, bf16[128,384]{1,0:T(8,128)(2,1)S(1)}, u32[]{:S(2)}, u32[]{:S(2)}) collective-permute-start(bf16[128,384]{1,0:T(8,128)(2,1)S(1)} %get-tuple-element.56), channel_id=1, source_target_pairs={{0,0},{1,1},{2,2},{3,3},{4,4},{5,5},{6,6},{7,7},{8,72},{9,73},{10,... | collective-permute-start | bytes 294920 | tf_op jit(solution)/shard_map/ppermute | solution.py:91
  (107 shorter events, 53.8 us)
Async XLA Ops:
  1.4 11.2 %collective-permute-start.13 = (bf16[1536,128]{1,0:T(8,128)(2,1)S(1)}, bf16[1536,128]{1,0:T(8,128)(2,1)S(1)}, u32[]{:S(2)}, u32[]{:S(2)}) collective-permute-start(bf16[1536,128]{1,0:T(8,128)(2,1)S(1)} %get-tuple-element.49), channel_id=1, source_target_pairs={{0,2},{2,4},{4,6},{6,8},{8,10},{10,12},{12,14},{14,0},{128,142},{1... | collective-permute-start | bytes 1179656 | tf_op jit(solution)/shard_map/ppermute | solution.py:63
  8.6 12.4 %collective-permute-start = (bf16[1536,128]{1,0:T(8,128)(2,1)S(1)}, bf16[1536,128]{1,0:T(8,128)(2,1)S(1)}, u32[]{:S(2)}, u32[]{:S(2)}) collective-permute-start(bf16[1536,128]{1,0:T(8,128)(2,1)S(1)} %get-tuple-element.48), channel_id=1, source_target_pairs={{0,2},{2,4},{4,6},{6,8},{8,10},{10,12},{12,14},{14,0},{128,142},{1... | collective-permute-start | bytes 1179656 | tf_op jit(solution)/shard_map/ppermute | solution.py:63
  9.3 42.2 %collective-permute-start.5 = (bf16[1536,384]{1,0:T(8,128)(2,1)S(1)}, bf16[1536,384]{1,0:T(8,128)(2,1)}, u32[]{:S(2)}, u32[]{:S(2)}) collective-permute-start(bf16[1536,384]{1,0:T(8,128)(2,1)S(1)} %copy-done), channel_id=1, source_target_pairs={{0,1},{1,0},{2,3},{3,2},{4,5},{5,4},{6,7},{7,6},{8,9},{9,8},{10,11... | collective-permute-start | bytes 3538952 | tf_op jit(solution)/shard_map/ppermute | solution.py:53
  12.6 12.6 %collective-permute-start.14 = (bf16[1536,128]{1,0:T(8,128)(2,1)S(1)}, bf16[1536,128]{1,0:T(8,128)(2,1)}, u32[]{:S(2)}, u32[]{:S(2)}) collective-permute-start(bf16[1536,128]{1,0:T(8,128)(2,1)S(1)} %collective-permute-done.13), channel_id=1, source_target_pairs={{0,2},{2,4},{4,6},{6,8},{8,10},{10,12},{12,14},{14,0},{128,142},{1... | collective-permute-start | bytes 1179656 | tf_op jit(solution)/shard_map/ppermute | solution.py:63
  16.8 12.6 %collective-permute-start.25 = (bf16[1536,128]{1,0:T(8,128)(2,1)S(1)}, bf16[1536,128]{1,0:T(8,128)(2,1)S(1)}, u32[]{:S(2)}, u32[]{:S(2)}) collective-permute-start(bf16[1536,128]{1,0:T(8,128)(2,1)S(1)} %collective-permute-done.24), channel_id=1, source_target_pairs={{0,2},{2,4},{4,6},{6,8},{8,10},{10,12},{12,14},{14,0},{128,142},{1... | collective-permute-start | bytes 1179656 | tf_op jit(solution)/shard_map/ppermute | solution.py:63
  21.0 12.6 %collective-permute-start.1 = (bf16[1536,128]{1,0:T(8,128)(2,1)S(1)}, bf16[1536,128]{1,0:T(8,128)(2,1)S(1)}, u32[]{:S(2)}, u32[]{:S(2)}) collective-permute-start(bf16[1536,128]{1,0:T(8,128)(2,1)S(1)} %collective-permute-done), channel_id=1, source_target_pairs={{0,2},{2,4},{4,6},{6,8},{8,10},{10,12},{12,14},{14,0},{128,142},{1... | collective-permute-start | bytes 1179656 | tf_op jit(solution)/shard_map/ppermute | solution.py:63
  25.2 12.7 %collective-permute-start.15 = (bf16[1536,128]{1,0:T(8,128)(2,1)}, bf16[1536,128]{1,0:T(8,128)(2,1)}, u32[]{:S(2)}, u32[]{:S(2)}) collective-permute-start(bf16[1536,128]{1,0:T(8,128)(2,1)} %collective-permute-done.14), channel_id=1, source_target_pairs={{0,2},{2,4},{4,6},{6,8},{8,10},{10,12},{12,14},{14,0},{128,142},{1... | collective-permute-start | bytes 1179656 | tf_op jit(solution)/shard_map/ppermute | solution.py:63
  28.5 10.3 %collective-permute-start.4 = (f32[1536]{0:T(1024)S(1)}, f32[1536]{0:T(1024)S(1)}, u32[]{:S(2)}, u32[]{:S(2)}) collective-permute-start(f32[1536]{0:T(1024)S(1)} %copy-done.10), channel_id=1, source_target_pairs={{0,128},{128,0},{1,129},{129,1},{2,130},{130,2},{3,131},{131,3},{4... | collective-permute-start | bytes 18440 | tf_op jit(solution)/shard_map/ppermute | solution.py:48
  29.5 12.6 %collective-permute-start.26 = (bf16[1536,128]{1,0:T(8,128)(2,1)S(1)}, bf16[1536,128]{1,0:T(8,128)(2,1)S(1)}, u32[]{:S(2)}, u32[]{:S(2)}) collective-permute-start(bf16[1536,128]{1,0:T(8,128)(2,1)S(1)} %collective-permute-done.25), channel_id=1, source_target_pairs={{0,2},{2,4},{4,6},{6,8},{8,10},{10,12},{12,14},{14,0},{128,142},{1... | collective-permute-start | bytes 1179656 | tf_op jit(solution)/shard_map/ppermute | solution.py:63
  33.7 13.4 %collective-permute-start.2 = (bf16[1536,128]{1,0:T(8,128)(2,1)S(1)}, bf16[1536,128]{1,0:T(8,128)(2,1)S(1)}, u32[]{:S(2)}, u32[]{:S(2)}) collective-permute-start(bf16[1536,128]{1,0:T(8,128)(2,1)S(1)} %collective-permute-done.1), channel_id=1, source_target_pairs={{0,2},{2,4},{4,6},{6,8},{8,10},{10,12},{12,14},{14,0},{128,142},{1... | collective-permute-start | bytes 1179656 | tf_op jit(solution)/shard_map/ppermute | solution.py:63
  38.0 16.0 %collective-permute-start.16 = (bf16[1536,128]{1,0:T(8,128)(2,1)}, bf16[1536,128]{1,0:T(8,128)(2,1)S(1)}, u32[]{:S(2)}, u32[]{:S(2)}) collective-permute-start(bf16[1536,128]{1,0:T(8,128)(2,1)} %collective-permute-done.15), channel_id=1, source_target_pairs={{0,2},{2,4},{4,6},{6,8},{8,10},{10,12},{12,14},{14,0},{1,3},{3,5},... | collective-permute-start | bytes 1179656 | tf_op jit(solution)/shard_map/ppermute | solution.py:63
  42.1 13.2 %collective-permute-start.27 = (bf16[1536,128]{1,0:T(8,128)(2,1)S(1)}, bf16[1536,128]{1,0:T(8,128)(2,1)S(1)}, u32[]{:S(2)}, u32[]{:S(2)}) collective-permute-start(bf16[1536,128]{1,0:T(8,128)(2,1)S(1)} %collective-permute-done.26), channel_id=1, source_target_pairs={{128,142},{130,128},{132,130},{134,132},{136,134},{138,136},{140,1... | collective-permute-start | bytes 1179656 | tf_op jit(solution)/shard_map/ppermute | solution.py:63
  63.3 31.3 %collective-permute-start.28 = (bf16[256,768]{1,0:T(8,128)(2,1)S(1)}, bf16[256,768]{1,0:T(8,128)(2,1)S(1)}, u32[]{:S(2)}, u32[]{:S(2)}) collective-permute-start(bf16[256,768]{1,0:T(8,128)(2,1)S(1)} %convolution_convert_fusion.1), channel_id=1, source_target_pairs={{0,48},{16,0},{32,16},{48,32},{128,144},{144,160},{160,176},{176,1... | collective-permute-start | bytes 1179656 | tf_op jit(solution)/shard_map/ppermute | solution.py:81
  65.4 10.4 %collective-permute-start.29 = (bf16[256,768]{1,0:T(8,128)(2,1)S(1)}, bf16[256,768]{1,0:T(8,128)(2,1)S(1)}, u32[]{:S(2)}, u32[]{:S(2)}) collective-permute-start(bf16[256,768]{1,0:T(8,128)(2,1)S(1)} %convolution_convert_fusion), channel_id=1, source_target_pairs={{0,16},{16,32},{32,48},{48,0},{128,176},{144,128},{160,144},{176,1... | collective-permute-start | bytes 1179656 | tf_op jit(solution)/shard_map/ppermute | solution.py:80
  68.5 33.5 %collective-permute-start.17 = (bf16[256,768]{1,0:T(8,128)(2,1)}, bf16[256,768]{1,0:T(8,128)(2,1)}, u32[]{:S(2)}, u32[]{:S(2)}) collective-permute-start(bf16[256,768]{1,0:T(8,128)(2,1)} %convolution_convert_fusion.3), channel_id=1, source_target_pairs={{0,48},{16,0},{32,16},{48,32},{128,144},{144,160},{160,176},{176,1... | collective-permute-start | bytes 1179656 | tf_op jit(solution)/shard_map/ppermute | solution.py:81
  69.4 14.9 %collective-permute-start.18 = (bf16[256,768]{1,0:T(8,128)(2,1)S(1)}, bf16[256,768]{1,0:T(8,128)(2,1)S(1)}, u32[]{:S(2)}, u32[]{:S(2)}) collective-permute-start(bf16[256,768]{1,0:T(8,128)(2,1)S(1)} %convolution_convert_fusion.2), channel_id=1, source_target_pairs={{0,16},{16,32},{32,48},{48,0},{128,176},{144,128},{160,144},{176,1... | collective-permute-start | bytes 1179656 | tf_op jit(solution)/shard_map/ppermute | solution.py:80
  73.7 31.0 %collective-permute-start.6 = (bf16[256,768]{1,0:T(8,128)(2,1)}, bf16[256,768]{1,0:T(8,128)(2,1)}, u32[]{:S(2)}, u32[]{:S(2)}) collective-permute-start(bf16[256,768]{1,0:T(8,128)(2,1)} %convolution_convert_fusion.5), channel_id=1, source_target_pairs={{0,48},{16,0},{32,16},{48,32},{128,144},{144,160},{160,176},{176,1... | collective-permute-start | bytes 1179656 | tf_op jit(solution)/shard_map/ppermute | solution.py:81
  75.8 14.1 %collective-permute-start.7 = (bf16[256,768]{1,0:T(8,128)(2,1)S(1)}, bf16[256,768]{1,0:T(8,128)(2,1)S(1)}, u32[]{:S(2)}, u32[]{:S(2)}) collective-permute-start(bf16[256,768]{1,0:T(8,128)(2,1)S(1)} %convolution_convert_fusion.4), channel_id=1, source_target_pairs={{0,16},{16,32},{32,48},{48,0},{128,176},{144,128},{160,144},{176,1... | collective-permute-start | bytes 1179656 | tf_op jit(solution)/shard_map/ppermute | solution.py:80
  84.3 10.3 %collective-permute-start.30 = (bf16[256,768]{1,0:T(8,128)(2,1)S(1)}, bf16[256,768]{1,0:T(8,128)(2,1)S(1)}, u32[]{:S(2)}, u32[]{:S(2)}) collective-permute-start(bf16[256,768]{1,0:T(8,128)(2,1)S(1)} %fusion.8), channel_id=1, source_target_pairs={{0,16},{16,32},{32,48},{48,0},{128,176},{144,128},{160,144},{176,1... | collective-permute-start | bytes 1179656 | tf_op jit(solution)/shard_map/ppermute | solution.py:83
  89.9 12.1 %collective-permute-start.19 = (bf16[256,768]{1,0:T(8,128)(2,1)}, bf16[256,768]{1,0:T(8,128)(2,1)}, u32[]{:S(2)}, u32[]{:S(2)}) collective-permute-start(bf16[256,768]{1,0:T(8,128)(2,1)} %fusion.6), channel_id=1, source_target_pairs={{0,16},{16,32},{32,48},{48,0},{128,176},{144,128},{160,144},{176,1... | collective-permute-start | bytes 1179656 | tf_op jit(solution)/shard_map/ppermute | solution.py:83
  94.6 10.1 %collective-permute-start.8 = (bf16[256,768]{1,0:T(8,128)(2,1)}, bf16[256,768]{1,0:T(8,128)(2,1)}, u32[]{:S(2)}, u32[]{:S(2)}) collective-permute-start(bf16[256,768]{1,0:T(8,128)(2,1)} %fusion.4), channel_id=1, source_target_pairs={{0,16},{16,32},{32,48},{48,0},{128,176},{144,128},{160,144},{176,1... | collective-permute-start | bytes 1179656 | tf_op jit(solution)/shard_map/ppermute | solution.py:83
  96.8 38.2 %collective-permute-start.33 = (bf16[128,384]{1,0:T(8,128)(2,1)}, bf16[128,384]{1,0:T(8,128)(2,1)}, u32[]{:S(2)}, u32[]{:S(2)}) collective-permute-start(bf16[128,384]{1,0:T(8,128)(2,1)} %get-tuple-element.50), channel_id=1, source_target_pairs={{0,1},{1,0},{2,3},{3,2},{4,5},{5,4},{6,7},{7,6},{8,73},{9,72},{10,... | collective-permute-start | bytes 294920 | tf_op jit(solution)/shard_map/ppermute | solution.py:91
  108.5 11.5 %collective-permute-start.11 = (bf16[128,384]{1,0:T(8,128)(2,1)S(1)}, bf16[128,384]{1,0:T(8,128)(2,1)S(1)}, u32[]{:S(2)}, u32[]{:S(2)}) collective-permute-start(bf16[128,384]{1,0:T(8,128)(2,1)S(1)} %get-tuple-element.66), channel_id=1, source_target_pairs={{0,1},{1,0},{2,3},{3,2},{4,5},{5,4},{6,7},{7,6},{8,73},{9,72},{10,... | collective-permute-start | bytes 294920 | tf_op jit(solution)/shard_map/ppermute | solution.py:91
  121.8 11.2 %collective-permute-start.20 = (bf16[128,384]{1,0:T(8,128)(2,1)S(1)}, bf16[128,384]{1,0:T(8,128)(2,1)S(1)}, u32[]{:S(2)}, u32[]{:S(2)}) collective-permute-start(bf16[128,384]{1,0:T(8,128)(2,1)S(1)} %get-tuple-element.64), channel_id=1, source_target_pairs={{0,64},{1,65},{2,2},{3,3},{4,4},{5,5},{6,6},{7,7},{8,8},{9,9},{10,... | collective-permute-start | bytes 294920 | tf_op jit(solution)/shard_map/ppermute | solution.py:91
  (22 other events, 200.6 us)
